TPU v7x, 32 devices: a whole 2x2x4 slice. The times are simulated.
32 devices in a mesh: grp: 4 (over y, x), dev: 8 (over z, core).
Axes of the slice: x: 2, y: 2, z: 4, core: 2. Of those that a mesh axis runs over, the one named last changes fastest.
Arguments:
- source_id: int32 [524288], P(('grp', 'dev')), may hold values from 0 to 4095, as said below
- slot: int32 [524288], P(('grp', 'dev')), may hold values from 0 to 127, as said below
- owner: int32 [4096], replicated, may hold values from 0 to 4095, as said below
- counts: int32 [4096], P(('grp', 'dev')), may hold values from 1 to 128, as said below
- partials: float32 [5, 524288], P(None, ('grp', 'dev')), may hold values from -6 to 6
- residual: float32 [524288], P(('grp', 'dev')), may hold values from -6 to 6
- weight: float32 [524288], P(('grp', 'dev')), may hold values from 0.3 to 9
- prior: float32 [5, 4096], P(None, ('grp', 'dev')), may hold values from 0.5 to 4
Outputs:
- updates: float32 [5, 4096], P(None, ('grp', 'dev'))
- standardized: float32 [524288], P(('grp', 'dev'))
- norm: float32 [], replicated
Inputs may be any that keep to these rules, and one draw needn't show every extreme that they name: A permutation: source s stands at owner position owner[s], and position p belongs to device p // 128. `source_id`: the rows of one device stand in 32 aligned blocks of 512 rows; block k holds only rows whose source's owner position lies in device k's range. Over all rows, each pair of a source and a slot below 128 appears exactly once. A row is an observation when its slot is below its source's count, else padding. Each device's block of counts holds 128 at least once.
All inputs are finite; a program needn't handle non-finite values.
Results may differ from a plain program's by a relative error of at most 0.0003.
Values sent between devices are 32-bit elements; how exact they have to be, the bound alone decides.
No kernel may reach another device: no remote copies, remote signals or barrier semaphores. Data moves between devices by JAX's collectives and lax.ppermute only.
A program may use at most 64 MiB of HBM per device.

v0:
```python
import jax
import jax.numpy as jnp
from jax import lax
from jax.sharding import PartitionSpec as P


def solve_blocks(normal, moments):
    params = len(moments)
    factor = {}
    for column in range(params):
        running = normal[column][column]
        for earlier in range(column):
            running = running - factor[column, earlier] ** 2
        pivot_value = jnp.sqrt(running)
        factor[column, column] = pivot_value
        for target in range(column + 1, params):
            current = normal[target][column]
            for earlier in range(column):
                current = current - factor[target, earlier] * factor[column, earlier]
            factor[target, column] = current / pivot_value
    forward = []
    for target in range(params):
        current = moments[target]
        for earlier in range(target):
            current = current - factor[target, earlier] * forward[earlier]
        forward.append(current / factor[target, target])
    backward = [None] * params
    for target in reversed(range(params)):
        current = forward[target]
        for later in range(target + 1, params):
            current = current - factor[later, target] * backward[later]
        backward[target] = current / factor[target, target]
    return jnp.stack(backward)


def spread_rows(table, onehot):
    return lax.dot_general(table, onehot, (((1,), (1,)), ((), ())), precision=lax.Precision.HIGHEST)


def body(source_id, slot, owner, counts, partials, residual, weight, prior):
    group_count = lax.axis_size("grp")
    member_count = lax.axis_size("dev")
    params = partials.shape[0]
    fields_count = params + 2
    row_count = residual.shape[0]
    src_local = counts.shape[0]
    pad_slots = row_count // src_local
    block_rows = row_count // (group_count * member_count)
    position = owner[source_id]
    cell_index = position % src_local * pad_slots + slot
    fields = jnp.concatenate([partials, residual[None, :], weight[None, :]], axis=0)
    outgoing = (
        fields.reshape(fields_count, group_count, member_count, block_rows),
        cell_index.reshape(1, group_count, member_count, block_rows),
    )
    arrived, arrived_cell = (
        lax.all_to_all(
            lax.all_to_all(outgoing[0], "dev", split_axis=2, concat_axis=2, tiled=True),
            "grp",
            split_axis=1,
            concat_axis=1,
            tiled=True,
        ),
        lax.all_to_all(
            lax.all_to_all(outgoing[1], "dev", split_axis=2, concat_axis=2, tiled=True),
            "grp",
            split_axis=1,
            concat_axis=1,
            tiled=True,
        ),
    )
    arrived = arrived.reshape(fields_count, row_count)
    arrived_cell = arrived_cell.reshape(row_count)
    count_table = counts.astype(jnp.float32)[None, :]
    step_rows = min(row_count, 4096)
    step_count = row_count // step_rows
    columns = jnp.arange(src_local, dtype=jnp.int32)[None, :]
    pairs = [
        (first_idx, second_idx)
        for first_idx in range(params)
        for second_idx in range(first_idx, params)
    ]

    def block_view(index):
        start = index * step_rows
        piece = lax.dynamic_slice_in_dim(arrived, start, step_rows, 1)
        cells = lax.dynamic_slice_in_dim(arrived_cell, start, step_rows, 0)
        onehot = ((cells // pad_slots)[:, None] == columns).astype(jnp.float32)
        row_counts = spread_rows(count_table, onehot)[0]
        live = ((cells % pad_slots).astype(jnp.float32) < row_counts).astype(jnp.float32)
        return (piece, onehot, live)

    def accumulate(index, total):
        piece, onehot, live = block_view(index)
        slopes = piece[0:params]
        observed = piece[params]
        weighted = slopes * (piece[params + 1] * live)[None]
        terms = [weighted[first_idx] * slopes[second_idx] for first_idx, second_idx in pairs]
        terms = terms + [weighted[first_idx] * observed for first_idx in range(params)]
        stats = jnp.stack(terms)
        return total + jnp.dot(stats, onehot, precision=lax.Precision.HIGHEST)

    sums = lax.fori_loop(
        0, step_count, accumulate, jnp.zeros((len(pairs) + params, src_local), jnp.float32)
    )
    normal = [[None] * params for _ in range(params)]
    for pair_idx, (first_idx, second_idx) in enumerate(pairs):
        entry = sums[pair_idx]
        if first_idx == second_idx:
            entry = entry + prior[first_idx]
        normal[first_idx][second_idx] = entry
        normal[second_idx][first_idx] = entry
    moments = [sums[len(pairs) + first_idx] for first_idx in range(params)]
    updates = solve_blocks(normal, moments)

    def refit(index, fresh_rows):
        piece, onehot, live = block_view(index)
        fitted = jnp.sum(piece[0:params] * spread_rows(updates, onehot), axis=0)
        fresh_block = (piece[params] - fitted) * live
        return lax.dynamic_update_slice_in_dim(fresh_rows, fresh_block, index * step_rows, 0)

    fresh_cells = lax.fori_loop(0, step_count, refit, jnp.zeros((row_count,), jnp.float32))
    returned = lax.all_to_all(
        lax.all_to_all(
            fresh_cells.reshape(1, group_count, member_count, block_rows),
            "grp",
            split_axis=1,
            concat_axis=1,
            tiled=True,
        ),
        "dev",
        split_axis=2,
        concat_axis=2,
        tiled=True,
    )
    fresh = returned.reshape(row_count)
    totals = lax.psum(
        jnp.stack([jnp.sum(weight * fresh * fresh), jnp.sum(counts.astype(jnp.float32))]),
        ("grp", "dev"),
    )
    norm = jnp.sqrt(totals[0] / totals[1] + 1e-06)
    return (updates, fresh * jnp.sqrt(weight) / norm, norm)


def solution(mesh):
    in_specs = (
        P(("grp", "dev")),
        P(("grp", "dev")),
        P(),
        P(("grp", "dev")),
        P(None, ("grp", "dev")),
        P(("grp", "dev")),
        P(("grp", "dev")),
        P(None, ("grp", "dev")),
    )
    out_specs = (P(None, ("grp", "dev")), P(("grp", "dev")), P())
    return jax.shard_map(body, mesh=mesh, in_specs=in_specs, out_specs=out_specs, check_vma=False)
```

profile of v0, /device:TPU:0, one launch (start us, length us, event | category | flops | bytes accessed | tf_op | source)
XLA Modules:
  0.0 230.4 jit_solution(10447145855971860731)
XLA Ops:
  1.5 90.5 %gather_fusion = s32[16384]{0:T(1024)S(1)} fusion(s32[4096]{0:T(1024)S(1)} %copy-done, s32[16384]{0:T(1024)S(1)} %fusion.29), kind=kCustom, calls=%fused_computation | custom fusion | bytes 196608 | tf_op jit(solution)/shard_map/gather | solution.py:49
  92.8 6.5 %all-to-all-start.2 = ((s32[1,4,8,512]{3,1,0,2:T(4,128)}), s32[1,4,8,512]{3,1,0,2:T(4,128)S(1)}, u32[]{:S(2)}, u32[]{:S(2)}) async-start(s32[1,4,8,512]{3,1,0,2:T(4,128)} %copy.17), calls=%async_computation.2 | async-start | bytes 131072 | tf_op jit(solution)/shard_map/all_to_all | solution.py:65
  101.3 3.9 %all-to-all-done.2 = s32[1,4,8,512]{3,1,0,2:T(4,128)S(1)} async-done(((s32[1,4,8,512]{3,1,0,2:T(4,128)}), s32[1,4,8,512]{3,1,0,2:T(4,128)S(1)}, u32[]{:S(2)}, u32[]{:S(2)}) %all-to-all-start.2) | async-done | bytes 65568 | tf_op jit(solution)/shard_map/all_to_all | solution.py:65
  105.2 3.5 %all-to-all-start = ((f32[7,4,8,512]{3,1,0,2:T(4,128)}), f32[7,4,8,512]{3,1,0,2:T(4,128)S(1)}, u32[]{:S(2)}, u32[]{:S(2)}) async-start(f32[7,4,8,512]{3,1,0,2:T(4,128)} %copy.14), calls=%async_computation | async-start | bytes 917504 | tf_op jit(solution)/shard_map/all_to_all | solution.py:58
  109.4 13.2 %all-to-all-done = f32[7,4,8,512]{3,1,0,2:T(4,128)S(1)} async-done(((f32[7,4,8,512]{3,1,0,2:T(4,128)}), f32[7,4,8,512]{3,1,0,2:T(4,128)S(1)}, u32[]{:S(2)}, u32[]{:S(2)}) %all-to-all-start) | async-done | bytes 458784 | tf_op jit(solution)/shard_map/all_to_all | solution.py:58
  122.6 3.7 %all-to-all-start.3 = ((s32[1,4,8,512]{3,2,0,1:T(8,128)}), s32[1,4,8,512]{3,2,0,1:T(8,128)S(1)}, u32[]{:S(2)}, u32[]{:S(2)}) async-start(s32[1,4,8,512]{3,2,0,1:T(8,128)} %copy.18), calls=%async_computation.3 | async-start | bytes 131072 | tf_op jit(solution)/shard_map/all_to_all | solution.py:64
  127.2 3.9 %all-to-all-done.3 = s32[1,4,8,512]{3,2,0,1:T(8,128)S(1)} async-done(((s32[1,4,8,512]{3,2,0,1:T(8,128)}), s32[1,4,8,512]{3,2,0,1:T(8,128)S(1)}, u32[]{:S(2)}, u32[]{:S(2)}) %all-to-all-start.3) | async-done | bytes 65568 | tf_op jit(solution)/shard_map/all_to_all | solution.py:64
  131.1 3.5 %all-to-all-start.1 = ((f32[7,4,8,512]{3,2,0,1:T(8,128)}), f32[7,4,8,512]{3,2,0,1:T(8,128)S(1)}, u32[]{:S(2)}, u32[]{:S(2)}) async-start(f32[7,4,8,512]{3,2,0,1:T(8,128)} %copy.15), calls=%async_computation.1 | async-start | bytes 917504 | tf_op jit(solution)/shard_map/all_to_all | solution.py:57
  134.7 6.1 %all-to-all-done.1 = f32[7,4,8,512]{3,2,0,1:T(8,128)S(1)} async-done(((f32[7,4,8,512]{3,2,0,1:T(8,128)}), f32[7,4,8,512]{3,2,0,1:T(8,128)S(1)}, u32[]{:S(2)}, u32[]{:S(2)}) %all-to-all-start.1) | async-done | bytes 458784 | tf_op jit(solution)/shard_map/all_to_all | solution.py:57
  141.1 14.9 %while.33 = (s32[]{:T(128)}, f32[20,128]{1,0:T(8,128)S(1)}, f32[7,16384]{1,0:T(8,128)S(1)}, s32[16384]{0:T(1024)S(1)}, f32[1,128]{1,0:T(1,128)S(1)}, /*index=5*/...) while((s32[]{:T(128)}, f32[20,128]{1,0:T(8,128)S(1)}, ...), condition=%wide.region_1.2_spmd.clone, body=%wide.region_0.1_spmd.clone.sunk | while | flops 133391376 | bytes 2028365 | solution.py:103
  148.6 1.5 fusion.48
  152.4 1.5 fusion.48
  156.2 12.7 %while.32 = (s32[]{:T(128)}, f32[16384]{0:T(1024)S(1)}, s32[16384]{0:T(1024)S(1)}, f32[1,128]{1,0:T(1,128)S(1)}, f32[7,16384]{1,0:T(8,128)S(1)}, /*index=5*/f32[...) while((s32[]{:T(128)}, f32[16384]{0:T(1024)S(1)}, ...), condition=%wide.region_4.5_spmd.clone, body=%wide.region_2.4_spmd.clone.sunk | while | flops 38952968 | bytes 306359 | solution.py:122
  156.3 1.5 fusion.44
  157.8 1.5 fusion.45
  159.5 1.5 fusion.44
  161.0 1.5 fusion.45
  162.6 1.5 fusion.44
  164.1 1.5 fusion.45
  165.8 1.5 fusion.44
  169.0 7.4 %all_to_all.30 = f32[1,4,8,512]{3,2,0,1:T(8,128)S(1)} all-to-all(f32[1,4,8,512]{3,2,0,1:T(8,128)S(1)} %reshape.57), channel_id=1, replica_groups=mesh['grp'=4,'dev'=8] {'grp'}, dimensions={1} | all-to-all | bytes 131072 | tf_op jit(solution)/shard_map/all_to_all | solution.py:124
  177.1 3.4 %all-to-all-start.5 = ((f32[1,4,8,512]{3,1,0,2:T(4,128)}), f32[1,4,8,512]{3,1,0,2:T(4,128)S(1)}, u32[]{:S(2)}, u32[]{:S(2)}) async-start(f32[1,4,8,512]{3,1,0,2:T(4,128)} %copy.19), calls=%async_computation.5 | async-start | bytes 131072 | tf_op jit(solution)/shard_map/all_to_all | solution.py:123
  181.0 5.2 %all-to-all-done.5 = f32[1,4,8,512]{3,1,0,2:T(4,128)S(1)} async-done(((f32[1,4,8,512]{3,1,0,2:T(4,128)}), f32[1,4,8,512]{3,1,0,2:T(4,128)S(1)}, u32[]{:S(2)}, u32[]{:S(2)}) %all-to-all-start.5) | async-done | bytes 65568 | tf_op jit(solution)/shard_map/all_to_all | solution.py:123
  188.3 38.4 %psum.7 = f32[2]{0:T(128)S(1)} all-reduce(f32[2]{0:T(128)S(1)} %pad_maximum_fusion.1), channel_id=1, replica_groups=mesh['grp'=4,'dev'=8] {'grp','dev'}, use_global_device_ids=true, to_apply=%region_7.8 | all-reduce | flops 2 | bytes 16 | tf_op jit(solution)/shard_map/psum | solution.py:137
  (93 shorter events, 23.9 us)
Async XLA Ops:
  0.6 0.9 copy-start
  1.5 90.6 %copy-start.3 = (s32[16384]{0:T(1024)S(1)}, s32[16384]{0:T(1024)}, u32[]{:S(2)}) copy-start(s32[16384]{0:T(1024)} %param.13) | copy-start | bytes 196612
  92.1 7.2 %copy-start.2 = (f32[5,16384]{1,0:T(8,128)S(1)}, f32[5,16384]{1,0:T(8,128)}, u32[]{:S(2)}) copy-start(f32[5,16384]{1,0:T(8,128)} %param.16) | copy-start | bytes 983044
  92.8 6.7 %copy-start.4 = (f32[16384]{0:T(1024)S(1)}, f32[16384]{0:T(1024)}, u32[]{:S(2)}) copy-start(f32[16384]{0:T(1024)} %param.17) | copy-start | bytes 196612
  92.8 12.4 %all-to-all-start.2 = ((s32[1,4,8,512]{3,1,0,2:T(4,128)}), s32[1,4,8,512]{3,1,0,2:T(4,128)S(1)}, u32[]{:S(2)}, u32[]{:S(2)}) async-start(s32[1,4,8,512]{3,1,0,2:T(4,128)} %copy.17), calls=%async_computation.2 | async-start | bytes 131072 | tf_op jit(solution)/shard_map/all_to_all | solution.py:65
  99.3 0.8 copy-start.1
  105.2 17.3 %all-to-all-start = ((f32[7,4,8,512]{3,1,0,2:T(4,128)}), f32[7,4,8,512]{3,1,0,2:T(4,128)S(1)}, u32[]{:S(2)}, u32[]{:S(2)}) async-start(f32[7,4,8,512]{3,1,0,2:T(4,128)} %copy.14), calls=%async_computation | async-start | bytes 917504 | tf_op jit(solution)/shard_map/all_to_all | solution.py:58
  122.6 8.6 %all-to-all-start.3 = ((s32[1,4,8,512]{3,2,0,1:T(8,128)}), s32[1,4,8,512]{3,2,0,1:T(8,128)S(1)}, u32[]{:S(2)}, u32[]{:S(2)}) async-start(s32[1,4,8,512]{3,2,0,1:T(8,128)} %copy.18), calls=%async_computation.3 | async-start | bytes 131072 | tf_op jit(solution)/shard_map/all_to_all | solution.py:64
  127.2 7.4 %copy-start.7 = (s32[128]{0:T(128)S(1)}, s32[128]{0:T(128)}, u32[]{:S(2)}) copy-start(s32[128]{0:T(128)} %param.15) | copy-start | bytes 1540
  131.1 9.7 %all-to-all-start.1 = ((f32[7,4,8,512]{3,2,0,1:T(8,128)}), f32[7,4,8,512]{3,2,0,1:T(8,128)S(1)}, u32[]{:S(2)}, u32[]{:S(2)}) async-start(f32[7,4,8,512]{3,2,0,1:T(8,128)} %copy.15), calls=%async_computation.1 | async-start | bytes 917504 | tf_op jit(solution)/shard_map/all_to_all | solution.py:57
  141.1 14.9 %copy-start.6 = (f32[5,128]{1,0:T(8,128)S(1)}, f32[5,128]{1,0:T(8,128)}, u32[]{:S(2)}) copy-start(f32[5,128]{1,0:T(8,128)} %param.19) | copy-start | bytes 7684
  169.0 60.4 %copy-start.5 = (f32[5,128]{1,0:T(8,128)}, f32[5,128]{1,0:T(8,128)S(1)}, u32[]{:S(2)}) copy-start(f32[5,128]{1,0:T(8,128)S(1)} %get-tuple-element.647) | copy-start | bytes 7684
  177.1 9.2 %all-to-all-start.5 = ((f32[1,4,8,512]{3,1,0,2:T(4,128)}), f32[1,4,8,512]{3,1,0,2:T(4,128)S(1)}, u32[]{:S(2)}, u32[]{:S(2)}) async-start(f32[1,4,8,512]{3,1,0,2:T(4,128)} %copy.19), calls=%async_computation.5 | async-start | bytes 131072 | tf_op jit(solution)/shard_map/all_to_all | solution.py:123
where the time goes:
time: 231 us; the launch traced here: 230 us
  local copies, waits for them, and re-layouts  99.3 us (43%)
  blocking collectives  45.8 us (20%)
  waiting for transfers between devices  32.4 us (14%)
  matrix products  21.7 us (9%)
  starting transfers between devices  20.5 us (9%)
  other arithmetic  6.75 us (3%)
  between operations  3.41 us (1%)
    gather x1, local copies, waits for them, and re-layouts, body(): position = owner[source_id]  90.5 us
    psum x1, blocking collectives, body(): lax.psum(jnp.stack([jnp.sum(weight * fresh * fresh), jnp.sum(counts.astyp...  38.4 us
    dot_general x12, matrix products, spread_rows(): lax.dot_general(table, onehot, (((1,), (1,)), ((), ())), precision=lax.Pr...  17.7 us
    all_to_all x1, waiting for transfers between devices, body(): lax.all_to_all(outgoing[0], 'dev', split_axis=2, concat_axis=2, tiled=True)  13.2 us
    all_to_all x1, blocking collectives, body(): lax.all_to_all(fresh_cells.reshape(1, group_count, member_count, block_ro...  7.43 us
    all_to_all x1, starting transfers between devices, body(): lax.all_to_all(outgoing[1], 'dev', split_axis=2, concat_axis=2, tiled=True)  6.49 us
    all_to_all x1, waiting for transfers between devices, body(): lax.all_to_all(lax.all_to_all(outgoing[0], 'dev', split_axis=2, concat_ax...  6.14 us
    all_to_all x1, waiting for transfers between devices, body(): lax.all_to_all(lax.all_to_all(fresh_cells.reshape(1, group_count, member_...  5.25 us
  transfers between devices with their start and end apart: 5, of which 5 were waited for; matrix products, arithmetic and copies ran while one was open for 2% of the time, Pallas kernels for 0%

commit v1 on v0

v1 whole, which is shorter than its diff:
```python
import jax
import jax.numpy as jnp
from jax import lax
from jax.experimental import pallas as pl
from jax.experimental.pallas import tpu as pltpu
from jax.sharding import PartitionSpec as P

LANES = 128
SUB = 8


def pick_lanes(table, idx):
    return jnp.take_along_axis(table, idx, axis=1, mode="promise_in_bounds")


def pack_kernel(sid_ref, slot_ref, owner_ref, partials_ref, res_ref, wgt_ref, wire_ref, *, src_local, pad_slots):
    params = partials_ref.shape[0]
    table_tiles = owner_ref.shape[0] // SUB
    row_of = lax.broadcasted_iota(jnp.int32, (SUB, LANES), 0)

    def group(g, carry):
        base = pl.multiple_of(g * SUB, SUB)
        sid = sid_ref[pl.ds(base, SUB), :]
        low = sid % LANES
        high = sid // LANES

        def look(t, pos):
            tile = owner_ref[pl.ds(pl.multiple_of(t * SUB, SUB), SUB), :]
            for s in range(SUB):
                line = jnp.broadcast_to(tile[s : s + 1, :], (SUB, LANES))
                pos = jnp.where(high == t * SUB + s, pick_lanes(line, low), pos)
            return pos

        pos = jnp.zeros((SUB, LANES), jnp.int32)
        if table_tiles <= 4:
            for t in range(table_tiles):
                pos = look(t, pos)
        else:
            pos = lax.fori_loop(0, table_tiles, look, pos)
        cell = (pos % src_local * pad_slots + slot_ref[pl.ds(base, SUB), :]).astype(jnp.float32)
        res = res_ref[pl.ds(base, SUB), :]
        wgt = wgt_ref[pl.ds(base, SUB), :]
        for s in range(SUB):
            lane0 = pl.multiple_of((base + s) * LANES, LANES)
            slopes = partials_ref[:, pl.ds(lane0, LANES)]
            tile = jnp.concatenate([slopes, jnp.zeros((SUB - params, LANES), jnp.float32)], axis=0)
            tile = jnp.where(row_of == params, res[s : s + 1, :], tile)
            tile = jnp.where(row_of == params + 1, wgt[s : s + 1, :], tile)
            tile = jnp.where(row_of == params + 2, cell[s : s + 1, :], tile)
            wire_ref[base + s] = tile
        return carry

    lax.fori_loop(0, sid_ref.shape[0] // SUB, group, 0)


def solve_rows(normal, moments):
    params = len(moments)
    factor = {}
    for column in range(params):
        running = normal[column][column]
        for earlier in range(column):
            running = running - factor[column, earlier] ** 2
        pivot_value = jnp.sqrt(running)
        factor[column, column] = pivot_value
        for target in range(column + 1, params):
            current = normal[target][column]
            for earlier in range(column):
                current = current - factor[target, earlier] * factor[column, earlier]
            factor[target, column] = current / pivot_value
    forward = []
    for target in range(params):
        current = moments[target]
        for earlier in range(target):
            current = current - factor[target, earlier] * forward[earlier]
        forward.append(current / factor[target, target])
    backward = [None] * params
    for target in reversed(range(params)):
        current = forward[target]
        for later in range(target + 1, params):
            current = current - factor[later, target] * backward[later]
        backward[target] = current / factor[target, target]
    return backward


def owner_kernel(wire_ref, counts_ref, prior_ref, upd_ref, out_ref, acc_ref, live_ref, *, pad_slots, per):
    params = prior_ref.shape[0]
    chunks = wire_ref.shape[0]
    src_local = counts_ref.shape[1]
    row_of = lax.broadcasted_iota(jnp.int32, (SUB, LANES), 0)
    source_of = lax.broadcasted_iota(jnp.int32, (src_local, LANES), 0)
    counts = counts_ref[...]
    count_table = jnp.broadcast_to(counts, (SUB, src_local))
    acc_ref[...] = jnp.zeros_like(acc_ref)

    def cell_of(tile):
        cell = jnp.broadcast_to(tile[params + 2 : params + 3, :].astype(jnp.int32), (SUB, LANES))
        return cell // pad_slots, cell % pad_slots

    step = 8

    def gather_sums(index, carry):
        lefts, hots = [], []
        for s in range(step):
            chunk = index * step + s
            tile = wire_ref[chunk]
            source, slot = cell_of(tile)
            live = (slot < pick_lanes(count_table, source)).astype(jnp.float32)
            live_ref[chunk] = live
            scaled = tile * (tile[params + 1 : params + 2, :] * live)
            turn1 = jnp.concatenate([tile[1:params], tile[0:1], tile[params:]], axis=0)
            turn2 = jnp.concatenate([tile[2:params], tile[0:2], tile[params:]], axis=0)
            stats = jnp.concatenate(
                [scaled * tile, scaled * turn1, scaled * turn2, scaled * tile[params : params + 1, :]],
                axis=0,
            )
            first = stats.astype(jnp.bfloat16)
            rest = stats - first.astype(jnp.float32)
            second = rest.astype(jnp.bfloat16)
            third = (rest - second.astype(jnp.float32)).astype(jnp.bfloat16)
            lefts.append(jnp.concatenate([first, second, third], axis=0))
            hots.append((source_of == source[0:1, :]).astype(jnp.float32).astype(jnp.bfloat16))
        acc_ref[...] += lax.dot_general(
            jnp.concatenate(lefts, axis=1),
            jnp.concatenate(hots, axis=1),
            (((1,), (1,)), ((), ())),
            preferred_element_type=jnp.float32,
        )
        return carry

    lax.fori_loop(0, chunks // step, gather_sums, 0)
    width = 4 * SUB
    sums = acc_ref[0:width, :] + (acc_ref[width : 2 * width, :] + acc_ref[2 * width : 3 * width, :])
    normal = [[None] * params for _ in range(params)]
    for turn in range(3):
        for first_idx in range(params):
            second_idx = (first_idx + turn) % params
            entry = sums[turn * SUB + first_idx : turn * SUB + first_idx + 1, :]
            if turn == 0:
                entry = entry + prior_ref[first_idx : first_idx + 1, :]
            normal[first_idx][second_idx] = entry
            normal[second_idx][first_idx] = entry
    moments = [sums[3 * SUB + i : 3 * SUB + i + 1, :] for i in range(params)]
    solved = solve_rows(normal, moments)
    table = jnp.zeros((SUB, src_local), jnp.float32)
    for i in range(params):
        upd_ref[i : i + 1, :] = solved[i]
        table = jnp.where(row_of == i, solved[i], table)

    def refit(index, total):
        for s in range(step):
            chunk = index * step + s
            tile = wire_ref[chunk]
            source, _ = cell_of(tile)
            fitted = jnp.sum(
                jnp.where(row_of < params, tile * pick_lanes(table, source), 0.0), axis=0, keepdims=True
            )
            fresh = (tile[params : params + 1, :] - fitted) * live_ref[chunk][0:1, :]
            total = total + tile[params + 1 : params + 2, :] * fresh * fresh
            if per:
                out_ref[chunk // per, pl.ds(chunk % per, 1), :] = fresh
            else:
                out_ref[pl.ds(chunk, 1), :] = fresh
        return total

    total = lax.fori_loop(0, chunks // step, refit, jnp.zeros((1, LANES), jnp.float32))
    squares = jnp.sum(total, axis=1, keepdims=True)
    seen = jnp.sum(counts.astype(jnp.float32), axis=1, keepdims=True)
    lane_of = lax.broadcasted_iota(jnp.int32, (1, LANES), 1)
    line = jnp.where(lane_of == 0, squares, jnp.where(lane_of == 1, seen, 0.0))
    if per:
        for peer in range(out_ref.shape[0]):
            out_ref[peer, per : per + 1, :] = line
    else:
        out_ref[chunks : chunks + 1, :] = line


def finish_kernel(back_ref, wgt_ref, std_ref, norm_ref, *, per):
    peers = back_ref.shape[0]
    lines = jnp.sum(back_ref[:, per, :], axis=0, keepdims=True)
    lane_of = lax.broadcasted_iota(jnp.int32, (1, LANES), 1)
    squares = jnp.sum(jnp.where(lane_of == 0, lines, 0.0), axis=1, keepdims=True)
    seen = jnp.sum(jnp.where(lane_of == 1, lines, 0.0), axis=1, keepdims=True)
    norm = jnp.sqrt(squares / seen + 1e-06)
    norm_ref[...] = norm
    for peer in range(peers):
        rows = slice(peer * per, (peer + 1) * per)
        std_ref[rows, :] = back_ref[peer, 0:per, :] * jnp.sqrt(wgt_ref[rows, :]) / norm


def body(source_id, slot, owner, counts, partials, residual, weight, prior):
    axes = ("grp", "dev")
    peers = lax.axis_size("grp") * lax.axis_size("dev")
    params = partials.shape[0]
    row_count = residual.shape[0]
    src_local = counts.shape[0]
    pad_slots = row_count // src_local
    block_rows = row_count // peers
    chunks = row_count // LANES
    per = block_rows // LANES
    f32 = jnp.float32
    grid_of = lambda x: x.reshape(-1, LANES)
    wgt = grid_of(weight)
    wire = pl.pallas_call(
        lambda *refs: pack_kernel(*refs, src_local=src_local, pad_slots=pad_slots),
        out_shape=jax.ShapeDtypeStruct((chunks, SUB, LANES), f32),
        name="pack_rows",
    )(grid_of(source_id), grid_of(slot), grid_of(owner), partials, grid_of(residual), wgt)
    if per:
        arrived = lax.all_to_all(
            wire.reshape(peers, per, SUB, LANES), axes, split_axis=0, concat_axis=0, tiled=True
        ).reshape(chunks, SUB, LANES)
    else:
        parts = LANES // block_rows
        cut = wire.reshape(chunks, SUB, parts, block_rows).transpose(0, 2, 1, 3)
        cut = lax.all_to_all(
            cut.reshape(peers, SUB, block_rows), axes, split_axis=0, concat_axis=0, tiled=True
        )
        cut = cut.reshape(chunks, parts, SUB, block_rows).transpose(0, 2, 1, 3)
        arrived = cut.reshape(chunks, SUB, LANES)
    back_shape = (peers, per + 1, LANES) if per else (chunks + 1, LANES)
    updates, back = pl.pallas_call(
        lambda *refs: owner_kernel(*refs, pad_slots=pad_slots, per=per),
        out_shape=(
            jax.ShapeDtypeStruct((params, src_local), f32),
            jax.ShapeDtypeStruct(back_shape, f32),
        ),
        scratch_shapes=[
            pltpu.VMEM((12 * SUB, src_local), f32),
            pltpu.VMEM((chunks, SUB, LANES), f32),
        ],
        name="owner_fit",
    )(arrived, counts.reshape(1, -1), prior)
    if per:
        back = lax.all_to_all(back, axes, split_axis=0, concat_axis=0, tiled=True)
        standardized, norm = pl.pallas_call(
            lambda *refs: finish_kernel(*refs, per=per),
            out_shape=(
                jax.ShapeDtypeStruct((chunks, LANES), f32),
                jax.ShapeDtypeStruct((1, 1), f32),
            ),
            name="finish",
        )(back, wgt)
        return (updates, standardized.reshape(row_count), norm.reshape(()))
    line = jnp.broadcast_to(back[chunks, 0:2][None], (peers, 2))
    back = jnp.concatenate([back[:chunks].reshape(peers, block_rows), line], axis=1)
    back = lax.all_to_all(back, axes, split_axis=0, concat_axis=0, tiled=True)
    totals = jnp.sum(back[:, block_rows:], axis=0)
    norm = jnp.sqrt(totals[0] / totals[1] + 1e-06)
    fresh = back[:, :block_rows].reshape(row_count)
    return (updates, fresh * jnp.sqrt(weight) / norm, norm)


def solution(mesh):
    in_specs = (
        P(("grp", "dev")),
        P(("grp", "dev")),
        P(),
        P(("grp", "dev")),
        P(None, ("grp", "dev")),
        P(("grp", "dev")),
        P(("grp", "dev")),
        P(None, ("grp", "dev")),
    )
    out_specs = (P(None, ("grp", "dev")), P(("grp", "dev")), P())
    return jax.shard_map(body, mesh=mesh, in_specs=in_specs, out_specs=out_specs, check_vma=False)
```

time: 231 us -> 50.1 us (0.22)
  local copies, waits for them, and re-layouts: 99.3 us -> 0 us
  waiting for transfers between devices: 32.4 us -> 0 us
  matrix products: 21.7 us -> 0 us
  starting transfers between devices: 20.5 us -> 0 us
  Pallas kernels: 0 us -> 14 us
  blocking collectives: 45.8 us -> 35.1 us
  other arithmetic: 6.75 us -> 0 us
  between operations: 3.41 us -> 0.63 us
    gather x1 -> x0, local copies, waits for them, and re-layouts: 90.5 us -> none  [body(): position = owner[source_id]]
    psum x1 -> x0, blocking collectives: 38.4 us -> none  [body(): lax.psum(jnp.stack([jnp.sum(weight * fresh * fresh), jnp.sum(counts.astyp...]
    all_to_all x5 -> x0, waiting for transfers between devices: 32.4 us -> none  [the longest x1 13.2 us: body(): lax.all_to_all(outgoing[0], 'dev', split_axis=2, concat_axis=2, tiled=True)]
    all_to_all x1 -> x2, blocking collectives: 7.43 us -> 35.1 us  [the longest x1 23.7 us: body(): lax.all_to_all(wire.reshape(peers, per, SUB, LANES), axes, split_axis=0,...]
    dot_general x16 -> x0, matrix products: 21.7 us -> none  [the longest x12 17.7 us: spread_rows(): lax.dot_general(table, onehot, (((1,), (1,)), ((), ())), precision=lax.Pr...]
    all_to_all x5 -> x0, starting transfers between devices: 20.5 us -> none  [the longest x1 6.49 us: body(): lax.all_to_all(outgoing[1], 'dev', split_axis=2, concat_axis=2, tiled=True)]
    pallas_call x0 -> x3, Pallas kernels: none -> 14 us  [the longest x1 8.47 us: body(): pl.pallas_call(lambda *refs: owner_kernel(*refs, pad_slots=pad_slots, per...]
  transfers between devices with their start and end apart: 5 -> 0, of which waited for: 5 -> 0; matrix products, arithmetic and copies ran while one was open for 2% -> 0% of each run, Pallas kernels for 0% -> 0%
where the time goes in v1:
time: 50.1 us; the launch traced here: 49.7 us
  blocking collectives  35.1 us (70%)
  Pallas kernels  14 us (28%)
  between operations  0.63 us (1%)
    all_to_all x1, blocking collectives, body(): lax.all_to_all(wire.reshape(peers, per, SUB, LANES), axes, split_axis=0,...  23.7 us
    all_to_all x1, blocking collectives, body(): back = lax.all_to_all(back, axes, split_axis=0, concat_axis=0, tiled=True)  11.4 us
    pallas_call x1, Pallas kernels, body(): pl.pallas_call(lambda *refs: owner_kernel(*refs, pad_slots=pad_slots, per...  8.47 us
    pallas_call x1, Pallas kernels, body(): pl.pallas_call(lambda *refs: pack_kernel(*refs, src_local=src_local, pad_...  3.89 us
    pallas_call x1, Pallas kernels, body(): pl.pallas_call(lambda *refs: finish_kernel(*refs, per=per), out_shape=(ja...  1.66 us

profile of v1, /device:TPU:0, one launch (start us, length us, event | category | flops | bytes accessed | tf_op | source)
XLA Modules:
  0.0 49.7 jit_solution(11524892181101145825)
XLA Ops:
  0.6 3.9 %pack_rows.1 = f32[128,8,128]{2,1,0:T(8,128)} custom-call(s32[128,128]{1,0:T(8,128)} %bitcast.14, s32[128,128]{1,0:T(8,128)} %bitcast.15, s32[32,128]{1,0:T(8,128)} %bitcast.17, f32[5,16384]{1,0:T(8,128)} %refs_3_.1, f32[128,128]{1,0:T(8,128)} %bitcast.16, f32[128,128]{1,0:T(8,128)} %bitcast.12), custom_call_target="tpu_custom_call" | custom-call | tf_op jit(solution)/shard_map/pack_rows/pallas_call | solution.py:203
  4.5 23.7 %all_to_all.10 = f32[32,4,8,128]{3,2,1,0:T(8,128)} all-to-all(f32[32,4,8,128]{3,2,1,0:T(8,128)} %bitcast.11), channel_id=1, replica_groups=mesh['grp'=4,'dev'=8] {'grp','dev'}, dimensions={0} | all-to-all | bytes 1048576 | tf_op jit(solution)/shard_map/all_to_all | solution.py:209
  28.2 8.5 %owner_fit.1 = (f32[5,128]{1,0:T(8,128)}, f32[32,5,128]{2,1,0:T(8,128)}) custom-call(f32[128,8,128]{2,1,0:T(8,128)} %bitcast.10, s32[1,128]{1,0:T(1,128)} %bitcast.18, f32[5,128]{1,0:T(8,128)} %refs_2_.1), custom_call_target="tpu_custom_call" | custom-call | tf_op jit(solution)/shard_map/owner_fit/pallas_call | solution.py:221
  36.7 11.4 %all_to_all.11.refs_0_ = f32[32,5,128]{2,1,0:T(8,128)} all-to-all(f32[32,5,128]{2,1,0:T(8,128)} %get-tuple-element.8), channel_id=1, replica_groups=mesh['grp'=4,'dev'=8] {'grp','dev'}, dimensions={0} | all-to-all | bytes 163840 | tf_op jit(solution)/shard_map/all_to_all | solution.py:234
  48.1 1.7 %finish.1 = (f32[128,128]{1,0:T(8,128)}, f32[1,1]{1,0:T(1,128)}) custom-call(f32[32,5,128]{2,1,0:T(8,128)} %all_to_all.11.refs_0_, f32[128,128]{1,0:T(8,128)} %bitcast.13), custom_call_target="tpu_custom_call" | custom-call | tf_op jit(solution)/shard_map/finish/pallas_call | solution.py:235

commit v2 on v1

v2 whole, which is shorter than its diff:
```python
import jax
import jax.numpy as jnp
from jax import lax
from jax.experimental import pallas as pl
from jax.experimental.pallas import tpu as pltpu
from jax.sharding import PartitionSpec as P

LANES = 128
SUB = 8
QUAD = 4


def pick_lanes(table, idx):
    return jnp.take_along_axis(table, idx, axis=1, mode="promise_in_bounds")


def split_index(value, size):
    if size & (size - 1) == 0:
        return lax.shift_right_logical(value, size.bit_length() - 1), value & (size - 1)
    return lax.div(value, size), lax.rem(value, size)


def pack_kernel(sid_ref, slot_ref, owner_ref, partials_ref, res_ref, wgt_ref, wire_ref, *, src_local, pad_slots, compact):
    params = partials_ref.shape[0]
    bits = max(1, (src_local - 1).bit_length())
    fit = 31 // bits
    tiles = owner_ref.shape[0] // SUB
    row_of = lax.broadcasted_iota(jnp.int32, (SUB, LANES), 0)

    def merged(first, count):
        line = jnp.zeros((SUB, LANES), jnp.int32)
        for t in range(count):
            here = owner_ref[pl.ds(pl.multiple_of((first + t) * SUB, SUB), SUB), :]
            line = line | (split_index(here, src_local)[1] << (t * bits))
        return line

    def look(first, count, high, low, pos):
        packed = merged(first, count)
        tile_id, line_id = split_index(high, SUB)
        found = jnp.zeros((SUB, LANES), jnp.int32)
        for s in range(SUB):
            line = jnp.broadcast_to(packed[s : s + 1, :], (SUB, LANES))
            found = jnp.where(line_id == s, pick_lanes(line, low), found)
        turn = tile_id - first
        inside = (turn >= 0) & (turn < count)
        moved = lax.shift_right_logical(found, jnp.where(inside, turn, 0) * bits) & ((1 << bits) - 1)
        return jnp.where(inside, moved, pos)

    def group(g, carry):
        base = pl.multiple_of(g * SUB, SUB)
        high, low = split_index(sid_ref[pl.ds(base, SUB), :], LANES)
        pos = jnp.zeros((SUB, LANES), jnp.int32)
        whole = tiles // fit
        if whole <= 1:
            for t in range(whole):
                pos = look(t * fit, fit, high, low, pos)
        else:
            pos = lax.fori_loop(0, whole, lambda t, p: look(t * fit, fit, high, low, p), pos)
        if tiles % fit:
            pos = look(whole * fit, tiles % fit, high, low, pos)
        cell = (pos * pad_slots + slot_ref[pl.ds(base, SUB), :]).astype(jnp.float32)
        root = jnp.sqrt(wgt_ref[pl.ds(base, SUB), :])
        res = res_ref[pl.ds(base, SUB), :] * root
        built = []
        for s in range(SUB):
            lane0 = pl.multiple_of((base + s) * LANES, LANES)
            slopes = partials_ref[:, pl.ds(lane0, LANES)] * root[s : s + 1, :]
            tile = jnp.concatenate([slopes, jnp.zeros((SUB - params, LANES), jnp.float32)], axis=0)
            tile = jnp.where(row_of == params, res[s : s + 1, :], tile)
            built.append(jnp.where(row_of == params + 1, cell[s : s + 1, :], tile))
        if not compact:
            for s in range(SUB):
                wire_ref[base + s] = built[s]
            return carry
        for quad in range(SUB // QUAD):
            last = built[quad * QUAD + QUAD - 1]
            line0 = (g * (SUB // QUAD) + quad) * (2 * QUAD - 1)
            for c in range(QUAD - 1):
                tile = jnp.where(row_of == SUB - 1, last[QUAD + c : QUAD + c + 1, :], built[quad * QUAD + c])
                wire_ref[line0 + 2 * c] = tile[0:QUAD]
                wire_ref[line0 + 2 * c + 1] = tile[QUAD:]
            wire_ref[line0 + 2 * QUAD - 2] = last[0:QUAD]
        return carry

    lax.fori_loop(0, sid_ref.shape[0] // SUB, group, 0)


def solve_rows(normal, moments):
    params = len(moments)
    raw, factor, inverse = {}, {}, []
    for column in range(params):
        for target in range(column, params):
            current = normal[target][column]
            for earlier in range(column):
                current = current - factor[target, earlier] * raw[column, earlier]
            raw[target, column] = current
        inverse.append(1.0 / raw[column, column])
        for target in range(column + 1, params):
            factor[target, column] = raw[target, column] * inverse[column]
    forward = []
    for target in range(params):
        current = moments[target]
        for earlier in range(target):
            current = current - factor[target, earlier] * forward[earlier]
        forward.append(current)
    backward = [None] * params
    for target in reversed(range(params)):
        current = forward[target] * inverse[target]
        for later in range(target + 1, params):
            current = current - factor[later, target] * backward[later]
        backward[target] = current
    return backward


def owner_kernel(wire_ref, counts_ref, prior_ref, upd_ref, out_ref, acc_ref, rows_ref, src_ref, *, pad_slots, per, compact):
    params = prior_ref.shape[0]
    chunks = rows_ref.shape[0]
    src_local = counts_ref.shape[1]
    row_of = lax.broadcasted_iota(jnp.int32, (SUB, LANES), 0)
    source_of = lax.broadcasted_iota(jnp.int32, (src_local, LANES), 0)
    counts = counts_ref[...]
    count_table = jnp.broadcast_to(counts, (SUB, src_local))
    acc_ref[...] = jnp.zeros_like(acc_ref)
    step = SUB

    def tiles_of(index):
        if not compact:
            return [wire_ref[index * step + s] for s in range(step)]
        out = []
        for quad in range(step // QUAD):
            line0 = (index * (step // QUAD) + quad) * (2 * QUAD - 1)
            three = [
                jnp.concatenate([wire_ref[line0 + 2 * c], wire_ref[line0 + 2 * c + 1]], axis=0)
                for c in range(QUAD - 1)
            ]
            spare = [tile[SUB - 1 :, :] for tile in three]
            last = jnp.concatenate([wire_ref[line0 + 2 * QUAD - 2]] + spare + [spare[0]], axis=0)
            out += three + [last]
        return out

    def gather_sums(index, carry):
        lefts, hots = [], []
        for s, tile in enumerate(tiles_of(index)):
            chunk = index * step + s
            cell = jnp.broadcast_to(tile[params + 1 : params + 2, :].astype(jnp.int32), (SUB, LANES))
            source, slot = split_index(cell, pad_slots)
            rows = jnp.where(slot < pick_lanes(count_table, source), tile, 0.0)
            rows_ref[chunk] = rows
            src_ref[chunk] = source
            left = jnp.where(row_of < params, rows, rows[params : params + 1, :])
            turn = lambda shift: pltpu.roll(rows, shift, 0)
            right0 = jnp.where(row_of < params, rows, turn(5))
            right1 = jnp.where(row_of < 4, turn(7), jnp.where(row_of == 4, turn(4), turn(2)))
            right2 = jnp.where(row_of < 3, turn(6), turn(3))
            parts = [left * right0, left * right1, left * right2]
            pieces = []
            for _ in range(2):
                heads = [p.astype(jnp.bfloat16).astype(jnp.float32) for p in parts]
                pieces += heads
                parts = [p - h for p, h in zip(parts, heads)]
            lefts.append(jnp.concatenate(pieces + parts, axis=0).astype(jnp.bfloat16))
            hots.append((source_of == source[0:1, :]).astype(jnp.float32).astype(jnp.bfloat16))
        acc_ref[...] += lax.dot_general(
            jnp.concatenate(lefts, axis=1),
            jnp.concatenate(hots, axis=1),
            (((1,), (1,)), ((), ())),
            preferred_element_type=jnp.float32,
        )
        return carry

    lax.fori_loop(0, chunks // step, gather_sums, 0)
    width = 3 * SUB
    sums = acc_ref[0:width, :] + (acc_ref[width : 2 * width, :] + acc_ref[2 * width : 3 * width, :])
    line_at = lambda turn, row: sums[turn * SUB + row : turn * SUB + row + 1, :]
    normal = [[None] * params for _ in range(params)]
    for turn in range(3):
        for first_idx in range(params):
            second_idx = (first_idx + turn) % params
            entry = line_at(turn, first_idx)
            if turn == 0:
                entry = entry + prior_ref[first_idx : first_idx + 1, :]
            normal[first_idx][second_idx] = entry
            normal[second_idx][first_idx] = entry
    moments = [line_at(0, 5), line_at(0, 6), line_at(0, 7), line_at(1, 5), line_at(1, 6)]
    solved = solve_rows(normal, moments)
    table = jnp.where(row_of == params, 1.0, 0.0)
    for i in range(params):
        upd_ref[i : i + 1, :] = solved[i]
        table = jnp.where(row_of == i, -solved[i], table)

    def refit(index, total):
        for s in range(step):
            chunk = index * step + s
            fresh = jnp.sum(rows_ref[chunk] * pick_lanes(table, src_ref[chunk]), axis=0, keepdims=True)
            total = total + fresh * fresh
            out_ref[chunk + (chunk // per if per else 0)] = fresh
        return total

    total = lax.fori_loop(0, chunks // step, refit, jnp.zeros((1, LANES), jnp.float32))
    squares = jnp.sum(total, axis=1, keepdims=True)
    seen = jnp.sum(counts.astype(jnp.float32), axis=1, keepdims=True)
    lane_of = lax.broadcasted_iota(jnp.int32, (1, LANES), 1)
    line = jnp.where(lane_of == 0, squares, jnp.where(lane_of == 1, seen, 0.0))
    stride = per + 1 if per else chunks + 1
    for last in range(stride - 1, out_ref.shape[0], stride):
        out_ref[last] = line


def finish_kernel(back_ref, std_ref, norm_ref, *, per):
    stride = per + 1
    lines = [back_ref[last] for last in range(per, back_ref.shape[0], stride)]
    while len(lines) > 1:
        lines = [a + b for a, b in zip(lines[::2], lines[1::2])] + lines[len(lines) & ~1 :]
    lane_of = lax.broadcasted_iota(jnp.int32, (1, LANES), 1)
    squares = jnp.sum(jnp.where(lane_of == 0, lines[0], 0.0), axis=1, keepdims=True)
    seen = jnp.sum(jnp.where(lane_of == 1, lines[0], 0.0), axis=1, keepdims=True)
    norm = jnp.sqrt(squares / seen + 1e-06)
    norm_ref[...] = norm
    inverse = jnp.broadcast_to(1.0 / norm, (1, LANES))
    for chunk in range(std_ref.shape[0]):
        std_ref[chunk : chunk + 1, :] = back_ref[chunk + chunk // per] * inverse


def body(source_id, slot, owner, counts, partials, residual, weight, prior):
    axes = ("grp", "dev")
    peers = lax.axis_size("grp") * lax.axis_size("dev")
    params = partials.shape[0]
    row_count = residual.shape[0]
    src_local = counts.shape[0]
    pad_slots = row_count // src_local
    block_rows = row_count // peers
    chunks = row_count // LANES
    per = block_rows // LANES
    compact = per > 0 and per % QUAD == 0
    f32 = jnp.float32
    grid_of = lambda x: x.reshape(-1, LANES)
    send = lambda x: lax.all_to_all(x, axes, split_axis=0, concat_axis=0, tiled=True)
    vmem_spec = pl.BlockSpec(memory_space=pltpu.VMEM)
    wire_shape = (chunks // QUAD * (2 * QUAD - 1), QUAD, LANES) if compact else (chunks, SUB, LANES)
    wire = pl.pallas_call(
        lambda *refs: pack_kernel(*refs, src_local=src_local, pad_slots=pad_slots, compact=compact),
        out_shape=pltpu.VMEM(wire_shape, f32),
        name="pack_rows",
    )(grid_of(source_id), grid_of(slot), grid_of(owner), partials, grid_of(residual), grid_of(weight))
    if per:
        arrived = send(wire.reshape((peers, -1) + wire_shape[1:])).reshape(wire_shape)
    else:
        parts = LANES // block_rows
        cut = wire.reshape(chunks, SUB, parts, block_rows).transpose(0, 2, 1, 3)
        cut = send(cut.reshape(peers, SUB, block_rows))
        cut = cut.reshape(chunks, parts, SUB, block_rows).transpose(0, 2, 1, 3)
        arrived = cut.reshape(wire_shape)
    back_lines = peers * (per + 1) if per else chunks + 1
    updates, back = pl.pallas_call(
        lambda *refs: owner_kernel(*refs, pad_slots=pad_slots, per=per, compact=compact),
        out_shape=(
            jax.ShapeDtypeStruct((params, src_local), f32),
            pltpu.VMEM((back_lines, 1, LANES), f32),
        ),
        in_specs=[vmem_spec] * 3,
        scratch_shapes=[
            pltpu.VMEM((9 * SUB, src_local), f32),
            pltpu.VMEM((chunks, SUB, LANES), f32),
            pltpu.VMEM((chunks, SUB, LANES), jnp.int32),
        ],
        name="owner_fit",
    )(arrived, counts.reshape(1, -1), prior)
    if per:
        back = send(back.reshape(peers, per + 1, 1, LANES)).reshape(back_lines, 1, LANES)
        standardized, norm = pl.pallas_call(
            lambda *refs: finish_kernel(*refs, per=per),
            out_shape=(
                jax.ShapeDtypeStruct((chunks, LANES), f32),
                jax.ShapeDtypeStruct((1, 1), f32),
            ),
            in_specs=[vmem_spec],
            name="finish",
        )(back)
        return (updates, standardized.reshape(row_count), norm.reshape(()))
    back = back[:, 0, :]
    line = jnp.broadcast_to(back[chunks, 0:2][None], (peers, 2))
    back = send(jnp.concatenate([back[:chunks].reshape(peers, block_rows), line], axis=1))
    totals = jnp.sum(back[:, block_rows:], axis=0)
    norm = jnp.sqrt(totals[0] / totals[1] + 1e-06)
    return (updates, back[:, :block_rows].reshape(row_count) / norm, norm)


def solution(mesh):
    in_specs = (
        P(("grp", "dev")),
        P(("grp", "dev")),
        P(),
        P(("grp", "dev")),
        P(None, ("grp", "dev")),
        P(("grp", "dev")),
        P(("grp", "dev")),
        P(None, ("grp", "dev")),
    )
    out_specs = (P(None, ("grp", "dev")), P(("grp", "dev")), P())
    return jax.shard_map(body, mesh=mesh, in_specs=in_specs, out_specs=out_specs, check_vma=False)
```

time: 50.1 us -> 45 us (0.90)
  blocking collectives: 35.1 us -> 32 us
  Pallas kernels: 14 us -> 12.2 us
    all_to_all x2, blocking collectives: 35.1 us -> 32 us  [body(): lax.all_to_all(x, axes, split_axis=0, concat_axis=0, tiled=True)]
    pallas_call x1, Pallas kernels: 3.89 us -> 2.58 us  [body(): pl.pallas_call(lambda *refs: pack_kernel(*refs, src_local=src_local, pad_...]
    pallas_call x1, Pallas kernels: 8.47 us -> 7.94 us  [body(): pl.pallas_call(lambda *refs: owner_kernel(*refs, pad_slots=pad_slots, per...]
where the time goes in v2:
time: 45 us; the launch traced here: 44.8 us
  blocking collectives  32 us (71%)
  Pallas kernels  12.2 us (27%)
  between operations  0.64 us (1%)
    all_to_all x2, blocking collectives, body(): lax.all_to_all(x, axes, split_axis=0, concat_axis=0, tiled=True)  32 us
    pallas_call x1, Pallas kernels, body(): pl.pallas_call(lambda *refs: owner_kernel(*refs, pad_slots=pad_slots, per...  7.94 us
    pallas_call x1, Pallas kernels, body(): pl.pallas_call(lambda *refs: pack_kernel(*refs, src_local=src_local, pad_...  2.58 us
    pallas_call x1, Pallas kernels, body(): pl.pallas_call(lambda *refs: finish_kernel(*refs, per=per), out_shape=(ja...  1.67 us

profile of v2, /device:TPU:0, one launch (start us, length us, event | category | flops | bytes accessed | tf_op | source)
XLA Modules:
  0.0 44.8 jit_solution(10400347750527342785)
XLA Ops:
  0.6 2.6 %pack_rows.1 = f32[224,4,128]{2,1,0:T(4,128)S(1)} custom-call(s32[128,128]{1,0:T(8,128)} %bitcast.16, s32[128,128]{1,0:T(8,128)} %bitcast.17, s32[32,128]{1,0:T(8,128)} %bitcast.20, f32[5,16384]{1,0:T(8,128)} %refs_3_.1, f32[128,128]{1,0:T(8,128)} %bitcast.18, f32[128,128]{1,0:T(8,128)} %bitcast.19), custom_call_target="tpu_custom_call" | custom-call | tf_op jit(solution)/shard_map/pack_rows/pallas_call | solution.py:240
  3.2 22.1 %all_to_all.10 = f32[32,7,4,128]{3,2,1,0:T(4,128)} all-to-all(f32[32,7,4,128]{3,2,1,0:T(4,128)S(1)} %bitcast.12), channel_id=1, replica_groups=mesh['grp'=4,'dev'=8] {'grp','dev'}, dimensions={0} | all-to-all | bytes 917504 | tf_op jit(solution)/shard_map/all_to_all | solution.py:237
  25.3 7.9 %owner_fit.1 = (f32[5,128]{1,0:T(8,128)}, f32[160,1,128]{2,1,0:T(1,128)S(1)}) custom-call(f32[224,4,128]{2,1,0:T(4,128)} %bitcast.14, s32[1,128]{1,0:T(1,128)} %bitcast.21, f32[5,128]{1,0:T(8,128)} %refs_2_.1), custom_call_target="tpu_custom_call" | custom-call | tf_op jit(solution)/shard_map/owner_fit/pallas_call | solution.py:254
  33.2 9.9 %all_to_all.11 = f32[32,5,1,128]{3,2,1,0:T(1,128)} all-to-all(f32[32,5,1,128]{3,2,1,0:T(1,128)S(1)} %bitcast.13), channel_id=1, replica_groups=mesh['grp'=4,'dev'=8] {'grp','dev'}, dimensions={0} | all-to-all | bytes 163840 | tf_op jit(solution)/shard_map/all_to_all | solution.py:237
  43.1 1.7 %finish.1 = (f32[128,128]{1,0:T(8,128)}, f32[1,1]{1,0:T(1,128)}) custom-call(f32[160,1,128]{2,1,0:T(1,128)} %bitcast.15), custom_call_target="tpu_custom_call" | custom-call | tf_op jit(solution)/shard_map/finish/pallas_call | solution.py:270

commit v3 on v2

--- a/solution.py
+++ b/solution.py
@@ -8,6 +8,7 @@
 LANES = 128
 SUB = 8
 QUAD = 4
+STEP = 128
 
 
 def pick_lanes(table, idx):
@@ -82,7 +83,7 @@
             wire_ref[line0 + 2 * QUAD - 2] = last[0:QUAD]
         return carry
 
-    lax.fori_loop(0, sid_ref.shape[0] // SUB, group, 0)
+    lax.fori_loop(0, sid_ref.shape[0] // SUB, group, 0, unroll=16)
 
 
 def solve_rows(normal, moments):
@@ -121,7 +122,7 @@
     counts = counts_ref[...]
     count_table = jnp.broadcast_to(counts, (SUB, src_local))
     acc_ref[...] = jnp.zeros_like(acc_ref)
-    step = SUB
+    step = min(STEP, chunks)
 
     def tiles_of(index):
         if not compact:
@@ -250,6 +251,7 @@
         cut = send(cut.reshape(peers, SUB, block_rows))
         cut = cut.reshape(chunks, parts, SUB, block_rows).transpose(0, 2, 1, 3)
         arrived = cut.reshape(wire_shape)
+    arrived = pltpu.with_memory_space_constraint(arrived, pltpu.VMEM)
     back_lines = peers * (per + 1) if per else chunks + 1
     updates, back = pl.pallas_call(
         lambda *refs: owner_kernel(*refs, pad_slots=pad_slots, per=per, compact=compact),
@@ -267,6 +269,7 @@
     )(arrived, counts.reshape(1, -1), prior)
     if per:
         back = send(back.reshape(peers, per + 1, 1, LANES)).reshape(back_lines, 1, LANES)
+        back = pltpu.with_memory_space_constraint(back, pltpu.VMEM)
         standardized, norm = pl.pallas_call(
             lambda *refs: finish_kernel(*refs, per=per),
             out_shape=(

time: 45 us -> 37.8 us (0.84)
  Pallas kernels: 12.2 us -> 5.27 us
    pallas_call x1, Pallas kernels: 7.94 us -> 3.11 us  [body(): pl.pallas_call(lambda *refs: owner_kernel(*refs, pad_slots=pad_slots, per...]
    pallas_call x1, Pallas kernels: 2.58 us -> 1.39 us  [body(): pl.pallas_call(lambda *refs: pack_kernel(*refs, src_local=src_local, pad_...]
    pallas_call x1, Pallas kernels: 1.67 us -> 0.78 us  [body(): pl.pallas_call(lambda *refs: finish_kernel(*refs, per=per), out_shape=(ja...]
where the time goes in v3:
time: 37.8 us; the launch traced here: 37.5 us
  blocking collectives  31.6 us (84%)
  Pallas kernels  5.27 us (14%)
  between operations  0.64 us (2%)
    all_to_all x2, blocking collectives, body(): lax.all_to_all(x, axes, split_axis=0, concat_axis=0, tiled=True)  31.6 us
    pallas_call x1, Pallas kernels, body(): pl.pallas_call(lambda *refs: owner_kernel(*refs, pad_slots=pad_slots, per...  3.11 us
    pallas_call x1, Pallas kernels, body(): pl.pallas_call(lambda *refs: pack_kernel(*refs, src_local=src_local, pad_...  1.39 us
    pallas_call x1, Pallas kernels, body(): pl.pallas_call(lambda *refs: finish_kernel(*refs, per=per), out_shape=(ja...  0.78 us

profile of v3, /device:TPU:0, one launch (start us, length us, event | category | flops | bytes accessed | tf_op | source)
XLA Modules:
  0.0 37.5 jit_solution(1687902390754244209)
XLA Ops:
  0.6 1.4 %pack_rows.1 = f32[224,4,128]{2,1,0:T(4,128)S(1)} custom-call(s32[128,128]{1,0:T(8,128)} %bitcast.16, s32[128,128]{1,0:T(8,128)} %bitcast.17, s32[32,128]{1,0:T(8,128)} %bitcast.20, f32[5,16384]{1,0:T(8,128)} %refs_3_.1, f32[128,128]{1,0:T(8,128)} %bitcast.18, f32[128,128]{1,0:T(8,128)} %bitcast.19), custom_call_target="tpu_custom_call" | custom-call | tf_op jit(solution)/shard_map/pack_rows/pallas_call | solution.py:241
  2.0 22.0 %all_to_all.10 = f32[32,7,4,128]{3,2,1,0:T(4,128)S(1)} all-to-all(f32[32,7,4,128]{3,2,1,0:T(4,128)S(1)} %bitcast.13), channel_id=1, replica_groups=mesh['grp'=4,'dev'=8] {'grp','dev'}, dimensions={0} | all-to-all | bytes 917504 | tf_op jit(solution)/shard_map/all_to_all | solution.py:238
  24.0 3.1 %owner_fit.1 = (f32[5,128]{1,0:T(8,128)}, f32[160,1,128]{2,1,0:T(1,128)S(1)}) custom-call(f32[224,4,128]{2,1,0:T(4,128)S(1)} %bitcast.12, s32[1,128]{1,0:T(1,128)} %bitcast.21, f32[5,128]{1,0:T(8,128)} %refs_2_.1), custom_call_target="tpu_custom_call" | custom-call | tf_op jit(solution)/shard_map/owner_fit/pallas_call | solution.py:256
  27.1 9.6 %all_to_all.11 = f32[32,5,1,128]{3,2,1,0:T(1,128)S(1)} all-to-all(f32[32,5,1,128]{3,2,1,0:T(1,128)S(1)} %bitcast.15), channel_id=1, replica_groups=mesh['grp'=4,'dev'=8] {'grp','dev'}, dimensions={0} | all-to-all | bytes 163840 | tf_op jit(solution)/shard_map/all_to_all | solution.py:238
  36.7 0.8 %finish.1 = (f32[128,128]{1,0:T(8,128)}, f32[1,1]{1,0:T(1,128)}) custom-call(f32[160,1,128]{2,1,0:T(1,128)S(1)} %bitcast.14), custom_call_target="tpu_custom_call" | custom-call | tf_op jit(solution)/shard_map/finish/pallas_call | solution.py:273

commit v4 on v3

--- a/solution.py
+++ b/solution.py
@@ -9,6 +9,7 @@
 SUB = 8
 QUAD = 4
 STEP = 128
+PART = 32
 
 
 def pick_lanes(table, idx):
@@ -161,12 +162,13 @@
                 parts = [p - h for p, h in zip(parts, heads)]
             lefts.append(jnp.concatenate(pieces + parts, axis=0).astype(jnp.bfloat16))
             hots.append((source_of == source[0:1, :]).astype(jnp.float32).astype(jnp.bfloat16))
-        acc_ref[...] += lax.dot_general(
-            jnp.concatenate(lefts, axis=1),
-            jnp.concatenate(hots, axis=1),
-            (((1,), (1,)), ((), ())),
-            preferred_element_type=jnp.float32,
-        )
+        for first in range(0, step, PART):
+            acc_ref[...] += lax.dot_general(
+                jnp.concatenate(lefts[first : first + PART], axis=1),
+                jnp.concatenate(hots[first : first + PART], axis=1),
+                (((1,), (1,)), ((), ())),
+                preferred_element_type=jnp.float32,
+            )
         return carry
 
     lax.fori_loop(0, chunks // step, gather_sums, 0)

time: 37.8 us -> 37.9 us (level)
  no operation moved by 1% of the time
where the time goes in v4:
time: 37.9 us; the launch traced here: 37.6 us
  blocking collectives  31.6 us (83%)
  Pallas kernels  5.39 us (14%)
  between operations  0.64 us (2%)
    all_to_all x2, blocking collectives, body(): lax.all_to_all(x, axes, split_axis=0, concat_axis=0, tiled=True)  31.6 us
    pallas_call x1, Pallas kernels, body(): pl.pallas_call(lambda *refs: owner_kernel(*refs, pad_slots=pad_slots, per...  3.22 us
    pallas_call x1, Pallas kernels, body(): pl.pallas_call(lambda *refs: pack_kernel(*refs, src_local=src_local, pad_...  1.39 us
    pallas_call x1, Pallas kernels, body(): pl.pallas_call(lambda *refs: finish_kernel(*refs, per=per), out_shape=(ja...  0.78 us

profile of v4, /device:TPU:0, one launch (start us, length us, event | category | flops | bytes accessed | tf_op | source)
XLA Modules:
  0.0 37.6 jit_solution(2098595458803795480)
XLA Ops:
  0.6 1.4 %pack_rows.1 = f32[224,4,128]{2,1,0:T(4,128)S(1)} custom-call(s32[128,128]{1,0:T(8,128)} %bitcast.16, s32[128,128]{1,0:T(8,128)} %bitcast.17, s32[32,128]{1,0:T(8,128)} %bitcast.20, f32[5,16384]{1,0:T(8,128)} %refs_3_.1, f32[128,128]{1,0:T(8,128)} %bitcast.18, f32[128,128]{1,0:T(8,128)} %bitcast.19), custom_call_target="tpu_custom_call" | custom-call | tf_op jit(solution)/shard_map/pack_rows/pallas_call | solution.py:243
  2.0 22.0 %all_to_all.10 = f32[32,7,4,128]{3,2,1,0:T(4,128)S(1)} all-to-all(f32[32,7,4,128]{3,2,1,0:T(4,128)S(1)} %bitcast.13), channel_id=1, replica_groups=mesh['grp'=4,'dev'=8] {'grp','dev'}, dimensions={0} | all-to-all | bytes 917504 | tf_op jit(solution)/shard_map/all_to_all | solution.py:240
  24.0 3.2 %owner_fit.1 = (f32[5,128]{1,0:T(8,128)}, f32[160,1,128]{2,1,0:T(1,128)S(1)}) custom-call(f32[224,4,128]{2,1,0:T(4,128)S(1)} %bitcast.12, s32[1,128]{1,0:T(1,128)} %bitcast.21, f32[5,128]{1,0:T(8,128)} %refs_2_.1), custom_call_target="tpu_custom_call" | custom-call | tf_op jit(solution)/shard_map/owner_fit/pallas_call | solution.py:258
  27.2 9.6 %all_to_all.11 = f32[32,5,1,128]{3,2,1,0:T(1,128)S(1)} all-to-all(f32[32,5,1,128]{3,2,1,0:T(1,128)S(1)} %bitcast.15), channel_id=1, replica_groups=mesh['grp'=4,'dev'=8] {'grp','dev'}, dimensions={0} | all-to-all | bytes 163840 | tf_op jit(solution)/shard_map/all_to_all | solution.py:240
  36.9 0.8 %finish.1 = (f32[128,128]{1,0:T(8,128)}, f32[1,1]{1,0:T(1,128)}) custom-call(f32[160,1,128]{2,1,0:T(1,128)S(1)} %bitcast.14), custom_call_target="tpu_custom_call" | custom-call | tf_op jit(solution)/shard_map/finish/pallas_call | solution.py:275
